TPU v7x, 32 devices: a whole 2x2x4 slice. The times are simulated.
32 devices in a mesh: space: 8 (over y, x, core), sect: 4 (over z).
Axes of the slice: x: 2, y: 2, z: 4, core: 2. Of those that a mesh axis runs over, the one named last changes fastest.
Arguments:
- density: float32 [24, 128, 2048], P('space', 'sect'), may hold values from 0.05 to 1
- velocity: float32 [24, 2048], P('space'), may hold values from -0.9 to 0.9
- kernel: float32 [128, 128], replicated, may hold values from 0.00078125 to 0.0078125
- split: float32 [128, 128], replicated, may hold values from 0 to 1
- target: int32 [128, 128], replicated, may hold values from 0 to 126, as said below
Outputs:
- updated: float32 [24, 128, 2048], P('space', 'sect')
Inputs may be any that keep to these rules, and one draw needn't show every extreme that they name: target is symmetric, and target[i][j] is at least min(max(i, j), 126).
All inputs are finite; a program needn't handle non-finite values.
Results may differ from a plain program's by a relative error of at most 0.00058.
Values may be sent and summed in bfloat16 or wider, within the bound.
A program may use at most 64 MiB of HBM per device.

v0:
```python
import jax
import jax.numpy as jnp
from jax import lax
from jax.experimental import pallas as pl
from jax.experimental.pallas import tpu as pltpu
from jax.sharding import PartitionSpec as P

STEPS = 4
LANES = 128
ROWS = 16
DEEP = 256


def unit_list(sections):
    blocks = sections // ROWS
    units = [(0, i, None) for i in range(ROWS)]
    for b in range(1, blocks // 2):
        units += [(b, ROWS * b + r, ROWS * (blocks - b) + r) for r in range(ROWS)]
    half = blocks // 2
    units += [(half, ROWS * half + r, ROWS * half + ROWS // 2 + r) for r in range(ROWS // 2)]
    return units


def fold_tables(table, share, sections):
    blocks = sections // ROWS
    lane = lax.broadcasted_iota(jnp.int32, (ROWS, sections), 1)
    pieces = [table[:ROWS]]
    for b in range(1, blocks // 2):
        near = table[ROWS * b : ROWS * (b + 1)]
        far = table[ROWS * (blocks - b) : ROWS * (blocks - b + 1)]
        pieces.append(jnp.where(lane < ROWS * b, pltpu.roll(far, ROWS * b, 1), near))
    half = blocks // 2
    near = table[ROWS * half : ROWS * half + ROWS // 2]
    far = table[ROWS * half + ROWS // 2 : ROWS * (half + 1)]
    pieces.append(
        jnp.where(lane[: ROWS // 2] < ROWS * half, pltpu.roll(far, ROWS * half, 1), near)
    )
    return jnp.concatenate(pieces, axis=0)


def build_coefficients(kernel_ref, split_ref, target_ref, tt, bb, ww, coef):
    sections = kernel_ref.shape[0]
    beta = 0.5 * (kernel_ref[...] + kernel_ref[...].T)
    weight = 0.5 * (split_ref[...] + split_ref[...].T)
    row = lax.broadcasted_iota(jnp.int32, (sections, sections), 0)
    col = lax.broadcasted_iota(jnp.int32, (sections, sections), 1)
    share = jnp.where(col > row, 1.0, jnp.where(col == row, 0.5, 0.0)) * beta
    tt[...] = fold_tables(target_ref[...], None, sections)
    bb[...] = fold_tables(share, None, sections)
    ww[...] = fold_tables(weight, None, sections)
    ks = lax.broadcasted_iota(jnp.int32, (sections, sections), 0)

    def one(tile, carry):
        for part in range(DEEP // sections):
            unit = tile * (DEEP // sections) + part
            t = tt[pl.ds(unit, 1), :]
            b = bb[pl.ds(unit, 1), :]
            w = ww[pl.ds(unit, 1), :]
            low = b * w
            high = b * (1.0 - w)
            value = jnp.where(ks == t, low, jnp.where(ks == t + 1, high, 0.0))
            coef[tile, :, part * sections : (part + 1) * sections] = value.astype(jnp.bfloat16)
        return carry

    lax.fori_loop(0, coef.shape[0] - 1, one, 0)
    coef[coef.shape[0] - 1] = jnp.concatenate(
        [beta.astype(jnp.bfloat16), jnp.zeros((sections, sections), jnp.bfloat16)], axis=1
    )


def pair_tile(wide, low, tile, units, sections):
    blocks = []
    for part in range(DEEP // sections):
        b, near, far = units[tile * (DEEP // sections) + part]
        if far is not None:
            lead = jnp.broadcast_to(wide[far : far + 1, :], (ROWS, wide.shape[1])).astype(jnp.bfloat16)
            for start in range(sections - ROWS * b, sections, ROWS):
                blocks.append(lead * low[start : start + ROWS, :])
        lead = jnp.broadcast_to(wide[near : near + 1, :], (ROWS, wide.shape[1])).astype(jnp.bfloat16)
        for start in range(ROWS * b, sections, ROWS):
            blocks.append(lead * low[start : start + ROWS, :])
    return jnp.concatenate(blocks, axis=0)


def advance_all(state, speed, coef, tiles, shift):
    sections = state.shape[1]
    units = unit_list(sections)
    count = len(units) * sections // DEEP
    chunk = 2 * LANES if tiles % 2 == 0 else LANES
    engines = 2 if (tiles * LANES // chunk) % 2 == 0 else 1
    trips = tiles * LANES // (chunk * engines)

    def pads(slot):
        state[slot, :, :LANES] = pltpu.roll(
            state[slot, :, tiles * LANES : (tiles + 1) * LANES], shift % LANES, 1
        )
        state[slot, :, (tiles + 1) * LANES :] = pltpu.roll(
            state[slot, :, LANES : 2 * LANES], (LANES - shift) % LANES, 1
        )

    def finish(now, at, gain, rate):
        here = pl.ds(pl.multiple_of(at + LANES, LANES), chunk)
        before = pl.ds(pl.multiple_of(at, LANES), chunk)
        after = pl.ds(pl.multiple_of(at + 2 * LANES, LANES), chunk)
        s = state[now, :, here]
        v, u = speed[:, here], speed[:, before]
        flux = jnp.maximum(v, 0.0) * s + jnp.minimum(v, 0.0) * state[now, :, after]
        behind = jnp.maximum(u, 0.0) * state[now, :, before] + jnp.minimum(u, 0.0) * s
        state[1 - now, :, here] = s - (flux - behind) + (gain - s * rate)

    def step(index, carry):
        now = lax.rem(index, 2)
        pads(now)

        def trip(n, carry):
            def body():
                starts = [(n * engines + q) * chunk for q in range(engines)]
                wides, lows = [], []
                for q in range(engines):
                    here = pl.ds(pl.multiple_of(starts[q] + LANES, LANES), chunk)
                    wide = state.at[now, :, here]
                    wides.append(wide)
                    lows.append(wide[...].astype(jnp.bfloat16))
                for tile in range(count):
                    for q in range(engines):
                        rhs = pair_tile(wides[q], lows[q], tile, units, sections)
                        pltpu.matmul_push_rhs(rhs, staging_register=tile % 2, mxu_index=q)
                        pltpu.matmul_acc_lhs(accs[2 * q], coef[tile], load_staged_rhs=tile % 2)
                for q in range(engines):
                    rhs = jnp.concatenate([lows[q]] * (DEEP // sections), axis=0)
                    pltpu.matmul_push_rhs(rhs, staging_register=count % 2, mxu_index=q)
                    pltpu.matmul_acc_lhs(accs[2 * q + 1], coef[count], load_staged_rhs=count % 2)
                for q in range(engines):
                    gain = pltpu.matmul_pop(accs[2 * q])
                    rate = pltpu.matmul_pop(accs[2 * q + 1])
                    finish(now, starts[q], gain, rate)

            def body_dot():
                start = n * chunk
                here = pl.ds(pl.multiple_of(start + LANES, LANES), chunk)
                wide = state.at[now, :, here]
                low = wide[...].astype(jnp.bfloat16)
                gain = jnp.zeros((sections, chunk), jnp.float32)
                for tile in range(count):
                    rhs = pair_tile(wide, low, tile, units, sections)
                    gain += jnp.dot(coef[tile], rhs, preferred_element_type=jnp.float32)
                rate = jnp.dot(
                    coef[count][:, :sections], low, preferred_element_type=jnp.float32
                )
                finish(now, start, gain, rate)

            if chunk == DEEP:
                body()
            else:
                body_dot()
            return carry

        lax.fori_loop(0, trips, trip, 0)
        return carry

    def every(*found):
        accs.extend(found)
        for acc in found:
            pltpu.matmul_pop(acc)
        lax.fori_loop(0, STEPS, step, 0)

    accs = []
    if chunk == DEEP:
        pl.run_scoped(
            every,
            *[
                pltpu.ACC(q)((sections, DEEP), jnp.float32)
                for q in range(engines)
                for _ in range(2)
            ],
        )
    else:
        every()


def compute_kernel(shift, x_ref, v_ref, kernel_ref, split_ref, target_ref, o_ref, state, speed, tt, bb, ww, coef):
    tiles = x_ref.shape[1] // LANES
    build_coefficients(kernel_ref, split_ref, target_ref, tt, bb, ww, coef)
    width = tiles * LANES
    state[0, :, LANES : LANES + width] = x_ref[...]
    speed[:, LANES : LANES + width] = v_ref[...]
    speed[:, :LANES] = pltpu.roll(v_ref[:, width - LANES :], shift % LANES, 1)
    speed[:, LANES + width :] = pltpu.roll(v_ref[:, :LANES], (LANES - shift) % LANES, 1)
    advance_all(state, speed, coef, tiles, shift)
    o_ref[...] = state[STEPS % 2, :, LANES : LANES + width]


def compute(x, v, kernel, split, target, shift):
    sections, width = x.shape
    units = len(unit_list(sections))
    vmem = pl.BlockSpec(memory_space=pltpu.VMEM)

    def call(*refs):
        compute_kernel(shift, *refs)

    return pl.pallas_call(
        call,
        out_shape=jax.ShapeDtypeStruct((sections, width), jnp.float32),
        in_specs=[vmem] * 5,
        out_specs=vmem,
        scratch_shapes=[
            pltpu.VMEM((2, sections, width + 2 * LANES), jnp.float32),
            pltpu.VMEM((1, width + 2 * LANES), jnp.float32),
            pltpu.VMEM((units, sections), jnp.int32),
            pltpu.VMEM((units, sections), jnp.float32),
            pltpu.VMEM((units, sections), jnp.float32),
            pltpu.VMEM((units * sections // DEEP + 1, sections, DEEP), jnp.bfloat16),
        ],
        name="coagulate",
    )(x, v, kernel, split, target)


def on_device(density, velocity, kernel, split, target):
    planes, block, width = density.shape
    sections = kernel.shape[0]
    space, sect = lax.axis_size("space"), lax.axis_size("sect")
    everyone = space * sect
    share = width // everyone
    groups = LANES // share
    tiles = planes * space // groups
    axes = ("space", "sect")

    sent = density.reshape(planes, block, everyone, share).transpose(2, 0, 1, 3)
    got = lax.all_to_all(sent, axes, 0, 0, tiled=True)
    got = got.reshape(space, sect, planes, block, share).transpose(1, 3, 0, 2, 4)
    got = got.reshape(sections, groups, tiles, share).transpose(0, 2, 1, 3)
    x = got.reshape(sections, tiles * LANES)

    vsent = velocity.reshape(planes, space, width // space).transpose(1, 0, 2)
    vgot = lax.all_to_all(vsent, "space", 0, 0, tiled=True).reshape(planes * space, width // space)
    v = lax.dynamic_slice_in_dim(vgot, lax.axis_index("sect") * share, share, 1)
    v = v.reshape(groups, tiles, share).transpose(1, 0, 2).reshape(1, tiles * LANES)

    y = compute(x, v, kernel, split, target, share)

    y = y.reshape(sections, tiles, groups, share).transpose(0, 2, 1, 3)
    y = y.reshape(sect, block, space, planes, share).transpose(2, 0, 3, 1, 4)
    y = y.reshape(everyone, planes, block, share)
    back = lax.all_to_all(y, axes, 0, 0, tiled=True)
    return back.transpose(1, 2, 0, 3).reshape(planes, block, width)


def solution(mesh):
    def run(*arrays):
        placed = (P("space", "sect", None), P("space", None), P(), P(), P())
        return jax.shard_map(
            on_device, mesh=mesh, in_specs=placed, out_specs=P("space", "sect", None), check_vma=False
        )(*arrays)

    def traced(*arrays):
        with jax.sharding.use_abstract_mesh(mesh.abstract_mesh):
            return run(*arrays)

    return traced
```

profile of v0, /device:TPU:0, one launch (start us, length us, event | category | flops | bytes accessed | tf_op | source)
XLA Modules:
  0.0 95.3 jit_solution(13148211021278105867)
XLA Ops:
  0.0 5.2 %all-to-all-start.1 = ((f32[8,3,256]{2,1,0:T(4,128)}), f32[8,3,256]{2,1,0:T(4,128)S(1)}, u32[]{:S(2)}, u32[]{:S(2)}) async-start(f32[8,3,256]{2,1,0:T(4,128)} %bitcast.31), calls=%async_computation.1 | async-start | bytes 65536 | tf_op jit(solution)/shard_map/all_to_all | solution.py:235
  5.2 1.8 %reshape.36 = f32[3,32,32,64]{3,2,1,0:T(8,128)S(1)} reshape(f32[3,32,2048]{2,1,0:T(8,128)} %param.5) | data formatting | bytes 1572864 | tf_op jit(solution)/shard_map/reshape | solution.py:228
  7.0 0.9 copy.30
  7.9 1.9 %reshape.48 = f32[32,1,6144]{2,1,0:T(1,128)} reshape(f32[32,3,32,64]{3,2,1,0:T(8,128)S(1)} %copy.30) | data formatting | bytes 1572864
  9.8 0.2 all-to-all-done.1
  10.0 6.1 %all-to-all-start = ((f32[32,1,6144]{2,1,0:T(1,128)}), f32[32,1,6144]{2,1,0:T(1,128)S(1)}, u32[]{:S(2)}, u32[]{:S(2)}) async-start(f32[32,1,6144]{2,1,0:T(1,128)} %reshape.48), calls=%async_computation | async-start | bytes 1572864 | tf_op jit(solution)/shard_map/all_to_all | solution.py:229
  16.2 0.1 constant_dynamic-slice_fusion
  16.3 0.7 reshape.43.refs_1_
  16.9 18.7 %all-to-all-done = f32[32,1,6144]{2,1,0:T(1,128)S(1)} async-done(((f32[32,1,6144]{2,1,0:T(1,128)}), f32[32,1,6144]{2,1,0:T(1,128)S(1)}, u32[]{:S(2)}, u32[]{:S(2)}) %all-to-all-start) | async-done | bytes 786464 | tf_op jit(solution)/shard_map/all_to_all | solution.py:229
  35.6 0.5 broadcast
  36.1 2.4 %reduce = f32[32,6144]{1,0:T(8,128)S(1)} reduce(f32[32,1,6144]{2,1,0:T(1,128)S(1)} %all-to-all-done, f32[]{:T(128)} %broadcast), dimensions={1}, to_apply=%all_to_all.9.reduce_sub_computation | reduce | bytes 1572868 | tf_op jit(solution)/shard_map/all_to_all | solution.py:229
  38.5 0.6 reshape.49
  39.1 0.2 copy.31
  39.3 0.4 copy.32
  39.8 1.1 %copy.35.refs_0_ = f32[128,1536]{1,0:T(8,128)} copy(f32[128,1536]{0,1:T(8,128)S(1)} %bitcast.28) | data formatting | bytes 1572864 | tf_op jit(solution)/shard_map/reshape | solution.py:232
  40.9 22.2 %coagulate.1 = f32[128,1536]{1,0:T(8,128)} custom-call(f32[128,1536]{1,0:T(8,128)} %copy.35.refs_0_, f32[1,1536]{1,0:T(1,128)} %reshape.43.refs_1_, f32[128,128]{1,0:T(8,128)} %refs_2_.1, f32[128,128]{1,0:T(8,128)} %refs_3_.1, s32[128,128]{1,0:T(8,128)} %refs_4_.1), custom_call_target="tpu_custom_call" | custom-call | tf_op jit(solution)/shard_map/coagulate/pallas_call | solution.py:201
  63.1 1.4 %copy.36 = f32[128,1536]{0,1:T(8,128)S(1)} copy(f32[128,1536]{1,0:T(8,128)} %coagulate.1) | data formatting | bytes 1572864 | tf_op jit(solution)/shard_map/coagulate/pallas_call | solution.py:201
  64.5 0.5 copy.37
  65.0 0.2 copy.38
  65.2 1.0 %reshape.50 = f32[32,1,6144]{2,1,0:T(1,128)S(1)} reshape(f32[32,3,32,64]{3,2,1,0:T(8,128)S(1)} %bitcast.25) | data formatting | bytes 1572864
  66.2 23.8 %all_to_all.15 = f32[32,1,6144]{2,1,0:T(1,128)S(1)} all-to-all(f32[32,1,6144]{2,1,0:T(1,128)S(1)} %reshape.50), channel_id=1, replica_groups=mesh['space'=8,'sect'=4] {'space','sect'}, dimensions={0} | all-to-all | bytes 1572864 | tf_op jit(solution)/shard_map/all_to_all | solution.py:244
  89.9 2.4 %reduce.1 = f32[32,6144]{1,0:T(8,128)S(1)} reduce(f32[32,1,6144]{2,1,0:T(1,128)S(1)} %all_to_all.15, f32[]{:T(128)} %broadcast), dimensions={1}, to_apply=%all_to_all.11.reduce_sub_computation | reduce | bytes 1572868 | tf_op jit(solution)/shard_map/all_to_all | solution.py:244
  92.3 0.6 reshape.51
  93.0 0.9 copy.39
  93.9 1.4 %reshape.47 = f32[3,32,2048]{2,1,0:T(8,128)} reshape(f32[3,32,32,64]{3,2,1,0:T(8,128)S(1)} %copy.39) | data formatting | bytes 1572864 | tf_op jit(solution)/shard_map/reshape | solution.py:245
  (3 shorter events, 0.0 us)
Async XLA Ops:
  0.0 10.0 %all-to-all-start.1 = ((f32[8,3,256]{2,1,0:T(4,128)}), f32[8,3,256]{2,1,0:T(4,128)S(1)}, u32[]{:S(2)}, u32[]{:S(2)}) async-start(f32[8,3,256]{2,1,0:T(4,128)} %bitcast.31), calls=%async_computation.1 | async-start | bytes 65536 | tf_op jit(solution)/shard_map/all_to_all | solution.py:235
  10.0 25.6 %all-to-all-start = ((f32[32,1,6144]{2,1,0:T(1,128)}), f32[32,1,6144]{2,1,0:T(1,128)S(1)}, u32[]{:S(2)}, u32[]{:S(2)}) async-start(f32[32,1,6144]{2,1,0:T(1,128)} %reshape.48), calls=%async_computation | async-start | bytes 1572864 | tf_op jit(solution)/shard_map/all_to_all | solution.py:229
where the time goes:
time: 96.7 us; the launch traced here: 95.3 us
  blocking collectives  23.8 us (25%)
  Pallas kernels  22.2 us (23%)
  waiting for transfers between devices  18.9 us (20%)
  local copies, waits for them, and re-layouts  14.2 us (15%)
  starting transfers between devices  11.3 us (12%)
  other arithmetic  4.82 us (5%)
    all_to_all x1, blocking collectives, on_device(): back = lax.all_to_all(y, axes, 0, 0, tiled=True)  23.8 us
    pallas_call x1, Pallas kernels, compute(): pl.pallas_call(call, out_shape=jax.ShapeDtypeStruct((sections, width), jn...  22.2 us
    all_to_all x1, waiting for transfers between devices, on_device(): got = lax.all_to_all(sent, axes, 0, 0, tiled=True)  18.7 us
    all_to_all x1, starting transfers between devices, on_device(): got = lax.all_to_all(sent, axes, 0, 0, tiled=True)  6.08 us
    all_to_all x1, starting transfers between devices, on_device(): lax.all_to_all(vsent, 'space', 0, 0, tiled=True)  5.2 us
    unnamed x4, local copies, waits for them, and re-layouts  4.07 us
    all_to_all x1, other arithmetic, on_device(): back = lax.all_to_all(y, axes, 0, 0, tiled=True)  2.41 us
    all_to_all x1, other arithmetic, on_device(): got = lax.all_to_all(sent, axes, 0, 0, tiled=True)  2.41 us
  transfers between devices with their start and end apart: 2, of which 2 were waited for; matrix products, arithmetic and copies ran while one was open for 6% of the time, Pallas kernels for 0%

commit v1 on v0

--- a/solution.py
+++ b/solution.py
@@ -215,6 +215,243 @@
     )(x, v, kernel, split, target)
 
 
+def swap_halves(first, second):
+    half = LANES // 2
+    left = lax.broadcasted_iota(jnp.int32, first.shape, 1) < half
+    return (
+        jnp.where(left, first, pltpu.roll(second, half, 1)),
+        jnp.where(left, pltpu.roll(first, half, 1), second),
+    )
+
+
+def peer_of(index, sect):
+    return {"space": index // sect, "sect": lax.rem(index, sect)}
+
+
+def greet(me, everyone, sect):
+    barrier = pltpu.get_barrier_semaphore()
+
+    def one(k, carry):
+        pl.semaphore_signal(
+            barrier,
+            inc=1,
+            device_id=peer_of(lax.rem(me + k, everyone), sect),
+            device_id_type=pl.DeviceIdType.MESH,
+        )
+        return carry
+
+    lax.fori_loop(1, everyone, one, 0)
+    return barrier
+
+
+def message(send, recv, ssem, rsem, me, peer, sect):
+    return pltpu.make_async_remote_copy(
+        src_ref=send.at[peer],
+        dst_ref=recv.at[me],
+        send_sem=ssem.at[peer],
+        recv_sem=rsem.at[me],
+        device_id=peer_of(peer, sect),
+        device_id_type=pl.DeviceIdType.MESH,
+    )
+
+
+def send_all(send, recv, ssem, rsem, me, everyone, sect):
+    def one(k, carry):
+        message(send, recv, ssem, rsem, me, lax.rem(me + k, everyone), sect).start()
+        return carry
+
+    lax.fori_loop(1, everyone, one, 0)
+    recv[me] = send[me]
+
+
+def wait_all(send, recv, ssem, rsem, me, everyone, sect):
+    def one(k, carry):
+        source = lax.rem(me + everyone - k, everyone)
+        pltpu.make_async_remote_copy(
+            src_ref=send.at[source],
+            dst_ref=recv.at[source],
+            send_sem=ssem.at[source],
+            recv_sem=rsem.at[source],
+            device_id=peer_of(source, sect),
+            device_id_type=pl.DeviceIdType.MESH,
+        ).wait_recv()
+        return carry
+
+    lax.fori_loop(1, everyone, one, 0)
+
+
+def wait_sent(send, recv, ssem, rsem, me, everyone, sect):
+    def one(k, carry):
+        message(send, recv, ssem, rsem, me, lax.rem(me + k, everyone), sect).wait_send()
+        return carry
+
+    lax.fori_loop(1, everyone, one, 0)
+
+
+MIDDLE = 0.525
+SCALE = 65536.0
+
+
+def coded(values):
+    return jnp.round((values - MIDDLE) * SCALE).astype(jnp.int32).astype(jnp.int16)
+
+
+def decoded(values):
+    return values.astype(jnp.int32).astype(jnp.float32) * (1.0 / SCALE) + MIDDLE
+
+
+def spread_kernel(space, sect, d_ref, v_ref, x_ref, vo_ref, send, recv, vsend, vrecv, ssem, rsem, vssem, vrsem):
+    planes, block, width = d_ref.shape
+    everyone = space * sect
+    mine, own = lax.axis_index("space"), lax.axis_index("sect")
+    me = mine * sect + own
+    barrier = greet(me, everyone, sect)
+    columns = width // LANES
+
+    def pack(c, carry):
+        here = pl.ds(pl.multiple_of(c * LANES, LANES), LANES)
+        for q in range(planes):
+            left, right = swap_halves(d_ref[q, :ROWS, here], d_ref[q, ROWS:, here])
+            send[2 * c, q] = coded(left)
+            send[2 * c + 1, q] = coded(right)
+        vsend[c, :planes, :] = v_ref[:, here]
+        return carry
+
+    lax.fori_loop(0, columns, pack, 0)
+    pl.semaphore_wait(barrier, everyone - 1)
+
+    def speeds(k, wait):
+        other = lax.rem(mine + k, space)
+        target = {"space": other, "sect": own}
+        copy = pltpu.make_async_remote_copy(
+            src_ref=vsend.at[(other * sect + own) // 2],
+            dst_ref=vrecv.at[mine],
+            send_sem=vssem.at[other],
+            recv_sem=vrsem.at[mine],
+            device_id=target,
+            device_id_type=pl.DeviceIdType.MESH,
+        )
+        if wait:
+            copy.wait_send()
+            pltpu.make_async_remote_copy(
+                src_ref=vsend.at[0],
+                dst_ref=vrecv.at[other],
+                send_sem=vssem.at[other],
+                recv_sem=vrsem.at[other],
+                device_id=target,
+                device_id_type=pl.DeviceIdType.MESH,
+            ).wait_recv()
+        else:
+            copy.start()
+
+    for k in range(1, space):
+        speeds(k, False)
+    send_all(send, recv, ssem, rsem, me, everyone, sect)
+    vrecv[mine] = vsend[me // 2]
+    for k in range(1, space):
+        speeds(k, True)
+    even = lax.rem(own, 2) == 0
+    for s in range(space // 2):
+        a, b = vrecv[s], vrecv[s + space // 2]
+        low, high = swap_halves(a, b)
+        both = jnp.where(even, low, high)
+        for q in range(planes):
+            t = s * planes + q
+            vo_ref[:, t * LANES : (t + 1) * LANES] = both[q : q + 1]
+    wait_all(send, recv, ssem, rsem, me, everyone, sect)
+    for s in range(space // 2):
+        for z in range(sect):
+            for q in range(planes):
+                t = s * planes + q
+                low, high = swap_halves(
+                    decoded(recv[s * sect + z, q]),
+                    decoded(recv[(s + space // 2) * sect + z, q]),
+                )
+                cols = slice(t * LANES, (t + 1) * LANES)
+                x_ref[z * block : z * block + ROWS, cols] = low
+                x_ref[z * block + ROWS : (z + 1) * block, cols] = high
+    wait_sent(send, recv, ssem, rsem, me, everyone, sect)
+
+
+def collect_kernel(space, sect, y_ref, o_ref, send, recv, ssem, rsem):
+    planes, block, width = o_ref.shape
+    everyone = space * sect
+    me = lax.axis_index("space") * sect + lax.axis_index("sect")
+    barrier = greet(me, everyone, sect)
+    for s in range(space // 2):
+        for z in range(sect):
+            for q in range(planes):
+                t = s * planes + q
+                cols = slice(t * LANES, (t + 1) * LANES)
+                low, high = swap_halves(
+                    y_ref[z * block : z * block + ROWS, cols],
+                    y_ref[z * block + ROWS : (z + 1) * block, cols],
+                )
+                send[s * sect + z, q] = low
+                send[(s + space // 2) * sect + z, q] = high
+    pl.semaphore_wait(barrier, everyone - 1)
+    send_all(send, recv, ssem, rsem, me, everyone, sect)
+    wait_all(send, recv, ssem, rsem, me, everyone, sect)
+
+    def unpack(c, carry):
+        here = pl.ds(pl.multiple_of(c * LANES, LANES), LANES)
+        for q in range(planes):
+            first, second = swap_halves(recv[2 * c, q], recv[2 * c + 1, q])
+            o_ref[q, :ROWS, here] = first
+            o_ref[q, ROWS:, here] = second
+        return carry
+
+    lax.fori_loop(0, width // LANES, unpack, 0)
+    wait_sent(send, recv, ssem, rsem, me, everyone, sect)
+
+
+def exchanged(density, velocity, kernel, split, target):
+    planes, block, width = density.shape
+    sections = kernel.shape[0]
+    space, sect = lax.axis_size("space"), lax.axis_size("sect")
+    everyone = space * sect
+    cells = width // everyone * planes * space
+    vmem = pl.BlockSpec(memory_space=pltpu.VMEM)
+    packet = [pltpu.VMEM((everyone, planes, ROWS, LANES), kind) for kind in (jnp.int16, jnp.float32)]
+
+    x, v = pl.pallas_call(
+        lambda *refs: spread_kernel(space, sect, *refs),
+        out_shape=(
+            jax.ShapeDtypeStruct((sections, cells), jnp.float32),
+            jax.ShapeDtypeStruct((1, cells), jnp.float32),
+        ),
+        in_specs=[vmem] * 2,
+        out_specs=(vmem, vmem),
+        scratch_shapes=[
+            packet[0],
+            packet[0],
+            pltpu.VMEM((width // LANES, 8, LANES), jnp.float32),
+            pltpu.VMEM((space, 8, LANES), jnp.float32),
+            pltpu.SemaphoreType.DMA((everyone,)),
+            pltpu.SemaphoreType.DMA((everyone,)),
+            pltpu.SemaphoreType.DMA((space,)),
+            pltpu.SemaphoreType.DMA((space,)),
+        ],
+        compiler_params=pltpu.CompilerParams(collective_id=0, has_side_effects=True),
+        name="spread",
+    )(density, velocity)
+    y = compute(x, v, kernel, split, target, width // everyone)
+    return pl.pallas_call(
+        lambda *refs: collect_kernel(space, sect, *refs),
+        out_shape=jax.ShapeDtypeStruct((planes, block, width), jnp.float32),
+        in_specs=[vmem],
+        out_specs=vmem,
+        scratch_shapes=[
+            packet[1],
+            packet[1],
+            pltpu.SemaphoreType.DMA((everyone,)),
+            pltpu.SemaphoreType.DMA((everyone,)),
+        ],
+        compiler_params=pltpu.CompilerParams(collective_id=1, has_side_effects=True),
+        name="collect",
+    )(y)
+
+
 def on_device(density, velocity, kernel, split, target):
     planes, block, width = density.shape
     sections = kernel.shape[0]
@@ -224,6 +461,8 @@
     groups = LANES // share
     tiles = planes * space // groups
     axes = ("space", "sect")
+    if 2 * share == LANES and block == 2 * ROWS and space % 2 == 0 and sect % 2 == 0 and planes <= 8:
+        return exchanged(density, velocity, kernel, split, target)
 
     sent = density.reshape(planes, block, everyone, share).transpose(2, 0, 1, 3)
     got = lax.all_to_all(sent, axes, 0, 0, tiled=True)

time: 96.7 us -> 70.7 us (0.73); the launches traced: 95.3 us -> 70.5 us
  Pallas kernels: 22.2 us -> 68.4 us
  blocking collectives: 23.8 us -> 0 us
  waiting for transfers between devices: 18.9 us -> 0 us
  local copies, waits for them, and re-layouts: 14.2 us -> 2.06 us
  starting transfers between devices: 11.3 us -> 0 us
  other arithmetic: 4.82 us -> 0 us
    pallas_call x0 -> x2, Pallas kernels: none -> 46.2 us  [the longest x1 26.1 us: exchanged(): pl.pallas_call(lambda *refs: collect_kernel(space, sect, *refs), out_shap...]
    all_to_all x1 -> x0, blocking collectives: 23.8 us -> none  [on_device(): back = lax.all_to_all(y, axes, 0, 0, tiled=True)]
    all_to_all x2 -> x0, waiting for transfers between devices: 18.9 us -> none  [the longest x1 18.7 us: on_device(): got = lax.all_to_all(sent, axes, 0, 0, tiled=True)]
    all_to_all x2 -> x0, starting transfers between devices: 11.3 us -> none  [the longest x1 6.08 us: on_device(): got = lax.all_to_all(sent, axes, 0, 0, tiled=True)]
    reshape x6 -> x0, local copies, waits for them, and re-layouts: 5.05 us -> none  [the longest x1 1.81 us: on_device(): sent = density.reshape(planes, block, everyone, share).transpose(2, 0, 1, 3)]
    all_to_all x2 -> x0, other arithmetic: 4.82 us -> none  [the longest x1 2.41 us: on_device(): back = lax.all_to_all(y, axes, 0, 0, tiled=True)]
    transpose x7 -> x0, local copies, waits for them, and re-layouts: 3.09 us -> none  [the longest x1 0.92 us: on_device(): sent = density.reshape(planes, block, everyone, share).transpose(2, 0, 1, 3)]
    unnamed x4 -> x1, local copies, waits for them, and re-layouts: 4.07 us -> 2.06 us
  transfers between devices with their start and end apart: 2 -> 0, of which waited for: 2 -> 0; matrix products, arithmetic and copies ran while one was open for 6% -> 0% of each run, Pallas kernels for 0% -> 0%
where the time goes in v1:
time: 70.7 us; the launch traced here: 70.5 us
  Pallas kernels  68.4 us (97%)
  local copies, waits for them, and re-layouts  2.06 us (3%)
    pallas_call x1, Pallas kernels, exchanged(): pl.pallas_call(lambda *refs: collect_kernel(space, sect, *refs), out_shap...  26.1 us
    pallas_call x1, Pallas kernels, compute(): pl.pallas_call(call, out_shape=jax.ShapeDtypeStruct((sections, width), jn...  22.2 us
    pallas_call x1, Pallas kernels, exchanged(): pl.pallas_call(lambda *refs: spread_kernel(space, sect, *refs), out_shape...  20.1 us
    unnamed x1, local copies, waits for them, and re-layouts  2.06 us

profile of v1, /device:TPU:0, one launch (start us, length us, event | category | flops | bytes accessed | tf_op | source)
XLA Modules:
  0.0 70.5 jit_solution(4421645908592895695)
XLA Ops:
  0.0 20.1 %spread.1 = (f32[128,1536]{1,0:T(8,128)}, f32[1,1536]{1,0:T(1,128)}) custom-call(f32[3,32,2048]{2,1,0:T(8,128)} %refs_0_.1, f32[3,2048]{1,0:T(4,128)} %refs_1_.1), custom_call_target="tpu_custom_call" | custom-call | tf_op jit(solution)/shard_map/spread/pallas_call | solution.py:417
  20.1 22.2 %coagulate.1.refs_0_ = f32[128,1536]{1,0:T(8,128)} custom-call(f32[128,1536]{1,0:T(8,128)} %get-tuple-element.7.refs_0_, f32[1,1536]{1,0:T(1,128)} %get-tuple-element.8.refs_1_, f32[128,128]{1,0:T(8,128)} %refs_2_.1, f32[128,128]{1,0:T(8,128)} %refs_3_.1, s32[128,128]{1,0:T(8,128)} %refs_4_.1), custom_call_target="tpu_custom_call" | custom-call | tf_op jit(solution)/shard_map/coagulate/pallas_call | solution.py:201
  42.3 26.1 %collect.1 = f32[3,32,2048]{2,1,0:T(8,128)} custom-call(f32[128,1536]{1,0:T(8,128)} %coagulate.1.refs_0_), custom_call_target="tpu_custom_call" | custom-call | tf_op jit(solution)/shard_map/collect/pallas_call | solution.py:439
  68.4 2.1 %copy.7 = f32[3,32,2048]{2,1,0:T(8,128)} copy(f32[3,32,2048]{2,1,0:T(8,128)} %collect.1) | data formatting | bytes 1572864

commit v2 on v1

--- a/solution.py
+++ b/solution.py
@@ -300,7 +300,26 @@
     return values.astype(jnp.int32).astype(jnp.float32) * (1.0 / SCALE) + MIDDLE
 
 
-def spread_kernel(space, sect, d_ref, v_ref, x_ref, vo_ref, send, recv, vsend, vrecv, ssem, rsem, vssem, vrsem):
+FLOOR = 0.03
+STEEP = 915.0 / 0.6931471805599453
+
+
+def coded_result(values):
+    code = jnp.log(1.0 + jnp.abs(values) * (1.0 / FLOOR)) * STEEP
+    return jnp.round(jnp.where(values < 0.0, -code, code)).astype(jnp.int32).astype(jnp.int16)
+
+
+def decoded_result(values):
+    code = values.astype(jnp.int32).astype(jnp.float32)
+    size = (jnp.exp(jnp.abs(code) * (1.0 / STEEP)) - 1.0) * FLOOR
+    return jnp.where(code < 0.0, -size, size)
+
+
+def fused_kernel(
+    space, sect, shift,
+    d_ref, v_ref, kernel_ref, split_ref, target_ref, back,
+    state, speed, tt, bb, ww, coef, send, recv, vsend, vrecv, ssem, rsem, vssem, vrsem, ssem2, rsem2,
+):
     planes, block, width = d_ref.shape
     everyone = space * sect
     mine, own = lax.axis_index("space"), lax.axis_index("sect")
@@ -344,65 +363,64 @@
         else:
             copy.start()
 
+    send_all(send, recv, ssem, rsem, me, everyone, sect)
     for k in range(1, space):
         speeds(k, False)
-    send_all(send, recv, ssem, rsem, me, everyone, sect)
     vrecv[mine] = vsend[me // 2]
+    build_coefficients(kernel_ref, split_ref, target_ref, tt, bb, ww, coef)
     for k in range(1, space):
         speeds(k, True)
     even = lax.rem(own, 2) == 0
     for s in range(space // 2):
-        a, b = vrecv[s], vrecv[s + space // 2]
-        low, high = swap_halves(a, b)
+        low, high = swap_halves(vrecv[s], vrecv[s + space // 2])
         both = jnp.where(even, low, high)
         for q in range(planes):
-            t = s * planes + q
-            vo_ref[:, t * LANES : (t + 1) * LANES] = both[q : q + 1]
+            t = s * planes + q + 1
+            speed[:, t * LANES : (t + 1) * LANES] = both[q : q + 1]
+    tiles = planes * space // 2
+    speed[:, :LANES] = pltpu.roll(speed[:, tiles * LANES : (tiles + 1) * LANES], shift, 1)
+    speed[:, (tiles + 1) * LANES :] = pltpu.roll(speed[:, LANES : 2 * LANES], shift, 1)
+
     wait_all(send, recv, ssem, rsem, me, everyone, sect)
     for s in range(space // 2):
         for z in range(sect):
             for q in range(planes):
-                t = s * planes + q
+                t = s * planes + q + 1
                 low, high = swap_halves(
                     decoded(recv[s * sect + z, q]),
                     decoded(recv[(s + space // 2) * sect + z, q]),
                 )
                 cols = slice(t * LANES, (t + 1) * LANES)
-                x_ref[z * block : z * block + ROWS, cols] = low
-                x_ref[z * block + ROWS : (z + 1) * block, cols] = high
+                state[0, z * block : z * block + ROWS, cols] = low
+                state[0, z * block + ROWS : (z + 1) * block, cols] = high
     wait_sent(send, recv, ssem, rsem, me, everyone, sect)
 
-
-def collect_kernel(space, sect, y_ref, o_ref, send, recv, ssem, rsem):
-    planes, block, width = o_ref.shape
-    everyone = space * sect
-    me = lax.axis_index("space") * sect + lax.axis_index("sect")
-    barrier = greet(me, everyone, sect)
+    advance_all(state, speed, coef, tiles, shift)
+
     for s in range(space // 2):
         for z in range(sect):
             for q in range(planes):
-                t = s * planes + q
+                t = s * planes + q + 1
                 cols = slice(t * LANES, (t + 1) * LANES)
                 low, high = swap_halves(
-                    y_ref[z * block : z * block + ROWS, cols],
-                    y_ref[z * block + ROWS : (z + 1) * block, cols],
+                    state[STEPS % 2, z * block : z * block + ROWS, cols],
+                    state[STEPS % 2, z * block + ROWS : (z + 1) * block, cols],
                 )
-                send[s * sect + z, q] = low
-                send[(s + space // 2) * sect + z, q] = high
-    pl.semaphore_wait(barrier, everyone - 1)
-    send_all(send, recv, ssem, rsem, me, everyone, sect)
-    wait_all(send, recv, ssem, rsem, me, everyone, sect)
-
-    def unpack(c, carry):
-        here = pl.ds(pl.multiple_of(c * LANES, LANES), LANES)
+                send[s * sect + z, q] = coded_result(low)
+                send[(s + space // 2) * sect + z, q] = coded_result(high)
+    send_all(send, back, ssem2, rsem2, me, everyone, sect)
+    wait_all(send, back, ssem2, rsem2, me, everyone, sect)
+    wait_sent(send, back, ssem2, rsem2, me, everyone, sect)
+
+
+def unpack_kernel(got, o_ref):
+    planes = o_ref.shape[0]
+    for c in range(o_ref.shape[2] // LANES):
+        here = slice(c * LANES, (c + 1) * LANES)
         for q in range(planes):
-            first, second = swap_halves(recv[2 * c, q], recv[2 * c + 1, q])
+            first, second = swap_halves(decoded_result(got[2 * c, q]), decoded_result(got[2 * c + 1, q]))
             o_ref[q, :ROWS, here] = first
             o_ref[q, ROWS:, here] = second
-        return carry
-
-    lax.fori_loop(0, width // LANES, unpack, 0)
-    wait_sent(send, recv, ssem, rsem, me, everyone, sect)
 
 
 def exchanged(density, velocity, kernel, split, target):
@@ -410,46 +428,47 @@
     sections = kernel.shape[0]
     space, sect = lax.axis_size("space"), lax.axis_size("sect")
     everyone = space * sect
-    cells = width // everyone * planes * space
+    share = width // everyone
+    cells = share * planes * space
+    units = len(unit_list(sections))
     vmem = pl.BlockSpec(memory_space=pltpu.VMEM)
-    packet = [pltpu.VMEM((everyone, planes, ROWS, LANES), kind) for kind in (jnp.int16, jnp.float32)]
-
-    x, v = pl.pallas_call(
-        lambda *refs: spread_kernel(space, sect, *refs),
-        out_shape=(
-            jax.ShapeDtypeStruct((sections, cells), jnp.float32),
-            jax.ShapeDtypeStruct((1, cells), jnp.float32),
-        ),
-        in_specs=[vmem] * 2,
-        out_specs=(vmem, vmem),
+    packet = (everyone, planes, ROWS, LANES)
+
+    got = pl.pallas_call(
+        lambda *refs: fused_kernel(space, sect, share, *refs),
+        out_shape=jax.ShapeDtypeStruct(packet, jnp.int16),
+        in_specs=[vmem] * 5,
+        out_specs=vmem,
         scratch_shapes=[
-            packet[0],
-            packet[0],
+            pltpu.VMEM((2, sections, cells + 2 * LANES), jnp.float32),
+            pltpu.VMEM((1, cells + 2 * LANES), jnp.float32),
+            pltpu.VMEM((units, sections), jnp.int32),
+            pltpu.VMEM((units, sections), jnp.float32),
+            pltpu.VMEM((units, sections), jnp.float32),
+            pltpu.VMEM((units * sections // DEEP + 1, sections, DEEP), jnp.bfloat16),
+            pltpu.VMEM(packet, jnp.int16),
+            pltpu.VMEM(packet, jnp.int16),
             pltpu.VMEM((width // LANES, 8, LANES), jnp.float32),
             pltpu.VMEM((space, 8, LANES), jnp.float32),
             pltpu.SemaphoreType.DMA((everyone,)),
             pltpu.SemaphoreType.DMA((everyone,)),
             pltpu.SemaphoreType.DMA((space,)),
             pltpu.SemaphoreType.DMA((space,)),
-        ],
-        compiler_params=pltpu.CompilerParams(collective_id=0, has_side_effects=True),
-        name="spread",
-    )(density, velocity)
-    y = compute(x, v, kernel, split, target, width // everyone)
-    return pl.pallas_call(
-        lambda *refs: collect_kernel(space, sect, *refs),
-        out_shape=jax.ShapeDtypeStruct((planes, block, width), jnp.float32),
-        in_specs=[vmem],
-        out_specs=vmem,
-        scratch_shapes=[
-            packet[1],
-            packet[1],
             pltpu.SemaphoreType.DMA((everyone,)),
             pltpu.SemaphoreType.DMA((everyone,)),
         ],
-        compiler_params=pltpu.CompilerParams(collective_id=1, has_side_effects=True),
-        name="collect",
-    )(y)
+        compiler_params=pltpu.CompilerParams(collective_id=0, has_side_effects=True),
+        name="soot",
+    )(density, velocity, kernel, split, target)
+    half = width // 2
+    return pl.pallas_call(
+        unpack_kernel,
+        grid=(2,),
+        out_shape=jax.ShapeDtypeStruct((planes, block, width), jnp.float32),
+        in_specs=[pl.BlockSpec((everyone // 2, planes, ROWS, LANES), lambda i: (i, 0, 0, 0))],
+        out_specs=pl.BlockSpec((planes, block, half), lambda i: (0, 0, i)),
+        name="unpack",
+    )(got)
 
 
 def on_device(density, velocity, kernel, split, target):

time: 70.7 us -> 53.5 us (0.76)
  Pallas kernels: 68.4 us -> 53.3 us
  local copies, waits for them, and re-layouts: 2.06 us -> 0 us
    pallas_call x3 -> x2, Pallas kernels: 68.4 us -> 53.3 us  [the longest x1 51.2 us: exchanged(): pl.pallas_call(lambda *refs: fused_kernel(space, sect, share, *refs), out...]
    unnamed x1 -> x0, local copies, waits for them, and re-layouts: 2.06 us -> none
where the time goes in v2:
time: 53.5 us; the launch traced here: 53.3 us
  Pallas kernels  53.3 us (100%)
    pallas_call x1, Pallas kernels, exchanged(): pl.pallas_call(lambda *refs: fused_kernel(space, sect, share, *refs), out...  51.2 us
    pallas_call x1, Pallas kernels, exchanged(): pl.pallas_call(unpack_kernel, grid=(2,), out_shape=jax.ShapeDtypeStruct((...  2.14 us

profile of v2, /device:TPU:0, one launch (start us, length us, event | category | flops | bytes accessed | tf_op | source)
XLA Modules:
  0.0 53.3 jit_solution(3857241771780111372)
XLA Ops:
  0.0 51.2 %soot.1.got = s16[32,3,16,128]{3,2,1,0:T(8,128)(2,1)} custom-call(f32[3,32,2048]{2,1,0:T(8,128)} %refs_0_.1, f32[3,2048]{1,0:T(4,128)} %refs_1_.1, f32[128,128]{1,0:T(8,128)} %refs_2_.1, f32[128,128]{1,0:T(8,128)} %refs_3_.1, s32[128,128]{1,0:T(8,128)} %refs_4_.1), custom_call_target="tpu_custom_call" | custom-call | tf_op jit(solution)/shard_map/soot/pallas_call | solution.py:437
  51.2 2.1 %unpack.1 = f32[3,32,2048]{2,1,0:T(8,128)} custom-call(s16[32,3,16,128]{3,2,1,0:T(8,128)(2,1)} %soot.1.got), custom_call_target="tpu_custom_call" | custom-call | tf_op jit(solution)/shard_map/unpack/pallas_call | solution.py:464

commit v3 on v2

--- a/solution.py
+++ b/solution.py
@@ -82,86 +82,68 @@
     return jnp.concatenate(blocks, axis=0)
 
 
-def advance_all(state, speed, coef, tiles, shift):
-    sections = state.shape[1]
+def advance_all(state, fresh, speed, coef, tiles, shift):
+    sections = state.shape[0]
     units = unit_list(sections)
     count = len(units) * sections // DEEP
     chunk = 2 * LANES if tiles % 2 == 0 else LANES
     engines = 2 if (tiles * LANES // chunk) % 2 == 0 else 1
     trips = tiles * LANES // (chunk * engines)
-
-    def pads(slot):
-        state[slot, :, :LANES] = pltpu.roll(
-            state[slot, :, tiles * LANES : (tiles + 1) * LANES], shift % LANES, 1
-        )
-        state[slot, :, (tiles + 1) * LANES :] = pltpu.roll(
-            state[slot, :, LANES : 2 * LANES], (LANES - shift) % LANES, 1
-        )
-
-    def finish(now, at, gain, rate):
-        here = pl.ds(pl.multiple_of(at + LANES, LANES), chunk)
-        before = pl.ds(pl.multiple_of(at, LANES), chunk)
-        after = pl.ds(pl.multiple_of(at + 2 * LANES, LANES), chunk)
-        s = state[now, :, here]
+    width = tiles * LANES
+
+    def pads():
+        state[:, :LANES] = pltpu.roll(state[:, width : width + LANES], shift % LANES, 1)
+        state[:, width + LANES :] = pltpu.roll(state[:, LANES : 2 * LANES], (LANES - shift) % LANES, 1)
+
+    def finish(at, gain, rate):
+        here = slice(at + LANES, at + LANES + chunk)
+        before = slice(at, at + chunk)
+        after = slice(at + 2 * LANES, at + 2 * LANES + chunk)
+        s = state[:, here]
         v, u = speed[:, here], speed[:, before]
-        flux = jnp.maximum(v, 0.0) * s + jnp.minimum(v, 0.0) * state[now, :, after]
-        behind = jnp.maximum(u, 0.0) * state[now, :, before] + jnp.minimum(u, 0.0) * s
-        state[1 - now, :, here] = s - (flux - behind) + (gain - s * rate)
+        flux = jnp.maximum(v, 0.0) * s + jnp.minimum(v, 0.0) * state[:, after]
+        behind = jnp.maximum(u, 0.0) * state[:, before] + jnp.minimum(u, 0.0) * s
+        fresh[:, before] = s - (flux - behind) + (gain - s * rate)
+
+    def trip(n):
+        starts = [(n * engines + q) * chunk for q in range(engines)]
+        wides = [state.at[:, at + LANES : at + LANES + chunk] for at in starts]
+        lows = [wide[...].astype(jnp.bfloat16) for wide in wides]
+        sums = accs[n % 2]
+        for tile in range(count):
+            for q in range(engines):
+                rhs = pair_tile(wides[q], lows[q], tile, units, sections)
+                pltpu.matmul_push_rhs(rhs, staging_register=tile % 2, mxu_index=q)
+                pltpu.matmul_acc_lhs(sums[2 * q], coef[tile], load_staged_rhs=tile % 2)
+        for q in range(engines):
+            rhs = jnp.concatenate([lows[q]] * (DEEP // sections), axis=0)
+            pltpu.matmul_push_rhs(rhs, staging_register=count % 2, mxu_index=q)
+            pltpu.matmul_acc_lhs(sums[2 * q + 1], coef[count], load_staged_rhs=count % 2)
+        for q in range(engines):
+            finish(starts[q], pltpu.matmul_pop(sums[2 * q]), pltpu.matmul_pop(sums[2 * q + 1]))
+
+    def trip_dot(n):
+        start = n * chunk
+        wide = state.at[:, start + LANES : start + LANES + chunk]
+        low = wide[...].astype(jnp.bfloat16)
+        gain = jnp.zeros((sections, chunk), jnp.float32)
+        for tile in range(count):
+            rhs = pair_tile(wide, low, tile, units, sections)
+            gain += jnp.dot(coef[tile], rhs, preferred_element_type=jnp.float32)
+        rate = jnp.dot(coef[count][:, :sections], low, preferred_element_type=jnp.float32)
+        finish(start, gain, rate)
 
     def step(index, carry):
-        now = lax.rem(index, 2)
-        pads(now)
-
-        def trip(n, carry):
-            def body():
-                starts = [(n * engines + q) * chunk for q in range(engines)]
-                wides, lows = [], []
-                for q in range(engines):
-                    here = pl.ds(pl.multiple_of(starts[q] + LANES, LANES), chunk)
-                    wide = state.at[now, :, here]
-                    wides.append(wide)
-                    lows.append(wide[...].astype(jnp.bfloat16))
-                for tile in range(count):
-                    for q in range(engines):
-                        rhs = pair_tile(wides[q], lows[q], tile, units, sections)
-                        pltpu.matmul_push_rhs(rhs, staging_register=tile % 2, mxu_index=q)
-                        pltpu.matmul_acc_lhs(accs[2 * q], coef[tile], load_staged_rhs=tile % 2)
-                for q in range(engines):
-                    rhs = jnp.concatenate([lows[q]] * (DEEP // sections), axis=0)
-                    pltpu.matmul_push_rhs(rhs, staging_register=count % 2, mxu_index=q)
-                    pltpu.matmul_acc_lhs(accs[2 * q + 1], coef[count], load_staged_rhs=count % 2)
-                for q in range(engines):
-                    gain = pltpu.matmul_pop(accs[2 * q])
-                    rate = pltpu.matmul_pop(accs[2 * q + 1])
-                    finish(now, starts[q], gain, rate)
-
-            def body_dot():
-                start = n * chunk
-                here = pl.ds(pl.multiple_of(start + LANES, LANES), chunk)
-                wide = state.at[now, :, here]
-                low = wide[...].astype(jnp.bfloat16)
-                gain = jnp.zeros((sections, chunk), jnp.float32)
-                for tile in range(count):
-                    rhs = pair_tile(wide, low, tile, units, sections)
-                    gain += jnp.dot(coef[tile], rhs, preferred_element_type=jnp.float32)
-                rate = jnp.dot(
-                    coef[count][:, :sections], low, preferred_element_type=jnp.float32
-                )
-                finish(now, start, gain, rate)
-
-            if chunk == DEEP:
-                body()
-            else:
-                body_dot()
-            return carry
-
-        lax.fori_loop(0, trips, trip, 0)
+        pads()
+        for n in range(trips):
+            (trip if chunk == DEEP else trip_dot)(n)
+        state[:, LANES : LANES + width] = fresh[...]
         return carry
 
     def every(*found):
-        accs.extend(found)
         for acc in found:
             pltpu.matmul_pop(acc)
+        accs.extend([found[: 2 * engines], found[2 * engines :]])
         lax.fori_loop(0, STEPS, step, 0)
 
     accs = []
@@ -170,6 +152,7 @@
             every,
             *[
                 pltpu.ACC(q)((sections, DEEP), jnp.float32)
+                for _ in range(2)
                 for q in range(engines)
                 for _ in range(2)
             ],
@@ -178,16 +161,16 @@
         every()
 
 
-def compute_kernel(shift, x_ref, v_ref, kernel_ref, split_ref, target_ref, o_ref, state, speed, tt, bb, ww, coef):
+def compute_kernel(shift, x_ref, v_ref, kernel_ref, split_ref, target_ref, o_ref, state, fresh, speed, tt, bb, ww, coef):
     tiles = x_ref.shape[1] // LANES
     build_coefficients(kernel_ref, split_ref, target_ref, tt, bb, ww, coef)
     width = tiles * LANES
-    state[0, :, LANES : LANES + width] = x_ref[...]
+    state[:, LANES : LANES + width] = x_ref[...]
     speed[:, LANES : LANES + width] = v_ref[...]
     speed[:, :LANES] = pltpu.roll(v_ref[:, width - LANES :], shift % LANES, 1)
     speed[:, LANES + width :] = pltpu.roll(v_ref[:, :LANES], (LANES - shift) % LANES, 1)
-    advance_all(state, speed, coef, tiles, shift)
-    o_ref[...] = state[STEPS % 2, :, LANES : LANES + width]
+    advance_all(state, fresh, speed, coef, tiles, shift)
+    o_ref[...] = fresh[...]
 
 
 def compute(x, v, kernel, split, target, shift):
@@ -204,7 +187,8 @@
         in_specs=[vmem] * 5,
         out_specs=vmem,
         scratch_shapes=[
-            pltpu.VMEM((2, sections, width + 2 * LANES), jnp.float32),
+            pltpu.VMEM((sections, width + 2 * LANES), jnp.float32),
+            pltpu.VMEM((sections, width), jnp.float32),
             pltpu.VMEM((1, width + 2 * LANES), jnp.float32),
             pltpu.VMEM((units, sections), jnp.int32),
             pltpu.VMEM((units, sections), jnp.float32),
@@ -318,7 +302,7 @@
 def fused_kernel(
     space, sect, shift,
     d_ref, v_ref, kernel_ref, split_ref, target_ref, back,
-    state, speed, tt, bb, ww, coef, send, recv, vsend, vrecv, ssem, rsem, vssem, vrsem, ssem2, rsem2,
+    state, fresh, speed, tt, bb, ww, coef, send, recv, vsend, vrecv, ssem, rsem, vssem, vrsem, ssem2, rsem2,
 ):
     planes, block, width = d_ref.shape
     everyone = space * sect
@@ -391,11 +375,11 @@
                     decoded(recv[(s + space // 2) * sect + z, q]),
                 )
                 cols = slice(t * LANES, (t + 1) * LANES)
-                state[0, z * block : z * block + ROWS, cols] = low
-                state[0, z * block + ROWS : (z + 1) * block, cols] = high
+                state[z * block : z * block + ROWS, cols] = low
+                state[z * block + ROWS : (z + 1) * block, cols] = high
     wait_sent(send, recv, ssem, rsem, me, everyone, sect)
 
-    advance_all(state, speed, coef, tiles, shift)
+    advance_all(state, fresh, speed, coef, tiles, shift)
 
     for s in range(space // 2):
         for z in range(sect):
@@ -403,8 +387,8 @@
                 t = s * planes + q + 1
                 cols = slice(t * LANES, (t + 1) * LANES)
                 low, high = swap_halves(
-                    state[STEPS % 2, z * block : z * block + ROWS, cols],
-                    state[STEPS % 2, z * block + ROWS : (z + 1) * block, cols],
+                    state[z * block : z * block + ROWS, cols],
+                    state[z * block + ROWS : (z + 1) * block, cols],
                 )
                 send[s * sect + z, q] = coded_result(low)
                 send[(s + space // 2) * sect + z, q] = coded_result(high)
@@ -440,7 +424,8 @@
         in_specs=[vmem] * 5,
         out_specs=vmem,
         scratch_shapes=[
-            pltpu.VMEM((2, sections, cells + 2 * LANES), jnp.float32),
+            pltpu.VMEM((sections, cells + 2 * LANES), jnp.float32),
+            pltpu.VMEM((sections, cells), jnp.float32),
             pltpu.VMEM((1, cells + 2 * LANES), jnp.float32),
             pltpu.VMEM((units, sections), jnp.int32),
             pltpu.VMEM((units, sections), jnp.float32),

time: 53.5 us -> 51.8 us (0.968)
  Pallas kernels: 53.3 us -> 51.6 us
    pallas_call x1, Pallas kernels: 51.2 us -> 49.5 us  [exchanged(): pl.pallas_call(lambda *refs: fused_kernel(space, sect, share, *refs), out...]
where the time goes in v3:
time: 51.8 us; the launch traced here: 51.6 us
  Pallas kernels  51.6 us (100%)
    pallas_call x1, Pallas kernels, exchanged(): pl.pallas_call(lambda *refs: fused_kernel(space, sect, share, *refs), out...  49.5 us
    pallas_call x1, Pallas kernels, exchanged(): pl.pallas_call(unpack_kernel, grid=(2,), out_shape=jax.ShapeDtypeStruct((...  2.14 us

profile of v3, /device:TPU:0, one launch (start us, length us, event | category | flops | bytes accessed | tf_op | source)
XLA Modules:
  0.0 51.6 jit_solution(10339907960517107618)
XLA Ops:
  0.0 49.5 %soot.1.got = s16[32,3,16,128]{3,2,1,0:T(8,128)(2,1)} custom-call(f32[3,32,2048]{2,1,0:T(8,128)} %refs_0_.1, f32[3,2048]{1,0:T(4,128)} %refs_1_.1, f32[128,128]{1,0:T(8,128)} %refs_2_.1, f32[128,128]{1,0:T(8,128)} %refs_3_.1, s32[128,128]{1,0:T(8,128)} %refs_4_.1), custom_call_target="tpu_custom_call" | custom-call | tf_op jit(solution)/shard_map/soot/pallas_call | solution.py:421
  49.5 2.1 %unpack.1 = f32[3,32,2048]{2,1,0:T(8,128)} custom-call(s16[32,3,16,128]{3,2,1,0:T(8,128)(2,1)} %soot.1.got), custom_call_target="tpu_custom_call" | custom-call | tf_op jit(solution)/shard_map/unpack/pallas_call | solution.py:449

commit v4 on v3

--- a/solution.py
+++ b/solution.py
@@ -82,7 +82,7 @@
     return jnp.concatenate(blocks, axis=0)
 
 
-def advance_all(state, fresh, speed, coef, tiles, shift):
+def advance_all(state, fresh, speed, coef, tiles, shift, emit=None):
     sections = state.shape[0]
     units = unit_list(sections)
     count = len(units) * sections // DEEP
@@ -144,7 +144,13 @@
         for acc in found:
             pltpu.matmul_pop(acc)
         accs.extend([found[: 2 * engines], found[2 * engines :]])
-        lax.fori_loop(0, STEPS, step, 0)
+        lax.fori_loop(0, STEPS - 1, step, 0)
+        pads()
+        done = 0
+        for n in range(trips):
+            (trip if chunk == DEEP else trip_dot)(n)
+            if emit is not None:
+                done = emit(done, (n + 1) * engines * chunk // LANES)
 
     accs = []
     if chunk == DEEP:
@@ -379,20 +385,35 @@
                 state[z * block + ROWS : (z + 1) * block, cols] = high
     wait_sent(send, recv, ssem, rsem, me, everyone, sect)
 
-    advance_all(state, fresh, speed, coef, tiles, shift)
-
-    for s in range(space // 2):
-        for z in range(sect):
-            for q in range(planes):
-                t = s * planes + q + 1
-                cols = slice(t * LANES, (t + 1) * LANES)
-                low, high = swap_halves(
-                    state[z * block : z * block + ROWS, cols],
-                    state[z * block + ROWS : (z + 1) * block, cols],
-                )
-                send[s * sect + z, q] = coded_result(low)
-                send[(s + space // 2) * sect + z, q] = coded_result(high)
-    send_all(send, back, ssem2, rsem2, me, everyone, sect)
+    def emit(done, ready):
+        last = ready // planes
+        for s in range(done, last):
+            for z in range(sect):
+                for q in range(planes):
+                    t = s * planes + q
+                    cols = slice(t * LANES, (t + 1) * LANES)
+                    low, high = swap_halves(
+                        fresh[z * block : z * block + ROWS, cols],
+                        fresh[z * block + ROWS : (z + 1) * block, cols],
+                    )
+                    send[s * sect + z, q] = coded_result(low)
+                    send[(s + space // 2) * sect + z, q] = coded_result(high)
+
+        def one(k, carry):
+            for first in (0, space // 2 * sect):
+                peer = first + k
+
+                @pl.when(peer != me)
+                def _():
+                    message(send, back, ssem2, rsem2, me, peer, sect).start()
+
+            return carry
+
+        lax.fori_loop(done * sect, last * sect, one, 0)
+        return last
+
+    advance_all(state, fresh, speed, coef, tiles, shift, emit)
+    back[me] = send[me]
     wait_all(send, back, ssem2, rsem2, me, everyone, sect)
     wait_sent(send, back, ssem2, rsem2, me, everyone, sect)
 
@@ -445,13 +466,13 @@
         compiler_params=pltpu.CompilerParams(collective_id=0, has_side_effects=True),
         name="soot",
     )(density, velocity, kernel, split, target)
-    half = width // 2
+    parts = 4
     return pl.pallas_call(
         unpack_kernel,
-        grid=(2,),
+        grid=(parts,),
         out_shape=jax.ShapeDtypeStruct((planes, block, width), jnp.float32),
-        in_specs=[pl.BlockSpec((everyone // 2, planes, ROWS, LANES), lambda i: (i, 0, 0, 0))],
-        out_specs=pl.BlockSpec((planes, block, half), lambda i: (0, 0, i)),
+        in_specs=[pl.BlockSpec((everyone // parts, planes, ROWS, LANES), lambda i: (i, 0, 0, 0))],
+        out_specs=pl.BlockSpec((planes, block, width // parts), lambda i: (0, 0, i)),
         name="unpack",
     )(got)
 

time: 51.8 us -> 48.6 us (0.938)
  the two profiles are of different devices: /device:TPU:0 before, /device:TPU:3 now
where the time goes in v4:
time: 48.6 us; the launch traced here: 48.3 us
  Pallas kernels  48.3 us (99%)
    pallas_call x1, Pallas kernels, exchanged(): pl.pallas_call(lambda *refs: fused_kernel(space, sect, share, *refs), out...  44.9 us
    pallas_call x1, Pallas kernels, exchanged(): pl.pallas_call(unpack_kernel, grid=(parts,), out_shape=jax.ShapeDtypeStru...  3.45 us

profile of v4, /device:TPU:3, one launch (start us, length us, event | category | flops | bytes accessed | tf_op | source)
XLA Modules:
  0.0 48.3 jit_solution(2688871461434354894)
XLA Ops:
  0.0 44.9 %soot.1.got = s16[32,3,16,128]{3,2,1,0:T(8,128)(2,1)} custom-call(f32[3,32,2048]{2,1,0:T(8,128)} %refs_0_.1, f32[3,2048]{1,0:T(4,128)} %refs_1_.1, f32[128,128]{1,0:T(8,128)} %refs_2_.1, f32[128,128]{1,0:T(8,128)} %refs_3_.1, s32[128,128]{1,0:T(8,128)} %refs_4_.1), custom_call_target="tpu_custom_call" | custom-call | tf_op jit(solution)/shard_map/soot/pallas_call | solution.py:442
  44.9 3.4 %unpack.1 = f32[3,32,2048]{2,1,0:T(8,128)} custom-call(s16[32,3,16,128]{3,2,1,0:T(8,128)(2,1)} %soot.1.got), custom_call_target="tpu_custom_call" | custom-call | tf_op jit(solution)/shard_map/unpack/pallas_call | solution.py:470
